TPU v7x, 256 devices: a whole 4x4x8 slice. The times are simulated.
256 devices in a mesh: pool: 8 (over y, core), expert: 32 (over x, z).
Axes of the slice: x: 4, y: 4, z: 8, core: 2. Of those that a mesh axis runs over, the one named last changes fastest.
Arguments:
- residual: bfloat16 [256, 2, 4096], P('expert'), may hold values from -6 to 6
- queries: bfloat16 [256, 2, 32, 128], P('expert', None, 'pool'), may hold values from -150 to 150
- kv_cache: bfloat16 [256, 512, 2, 2, 128], P('expert'), may hold values from -6 to 6
- kv_pages: bfloat16 [32, 32, 64, 2, 2, 128], P('pool', 'expert'), may hold values from -6 to 6
- cache_len: int32 [256], P('expert'), may hold values from 1 to 510, 65280 in all
- page_row: int32 [32, 32], P(None, 'expert'), may hold values from 0 to 7
- page_len: int32 [32, 32], P(None, 'expert'), may hold values from 1 to 64
- routes: int32 [256, 2, 8], P('expert'), may hold values from 0 to 63, all different within a row; in each aligned block of 16 rows (0 to 15, 16 to 31, ..., all dimensions but the last counted through in order) at most 3 rows name the same one
- route_weight: float32 [256, 2, 8], P('expert'), may hold values from 0.05 to 0.5
- out_weight: bfloat16 [4096, 4096], P('pool'), may hold values from -1.5 to 1.5
- gate_weight: bfloat16 [64, 4096, 1024], P('expert', None, 'pool'), may hold values from -0.09375 to 0.09375
- up_weight: bfloat16 [64, 4096, 1024], P('expert', None, 'pool'), may hold values from -0.09375 to 0.09375
- down_weight: bfloat16 [64, 1024, 4096], P('expert', 'pool'), may hold values from -0.375 to 0.375
Outputs:
- layer_out: bfloat16 [256, 2, 4096], P('expert')
Inputs may be any that keep to these rules, and one draw needn't show every extreme that they name: The row's two new tokens sit at positions cache_len and cache_len + 1 of its cache. The page belongs to row e * 8 + page_row of its group e. `routes`: a token names distinct experts; among the 16 new tokens of one device's rows no expert is named by more than 3 tokens.
All inputs are finite; a program needn't handle non-finite values. No bound on the sum of `cache_len` on one device may be relied on, other than what follows from the above.
Results may differ from a plain program's by a relative error of at most 0.028.
Values may be sent and summed in bfloat16 or wider, within the bound.
A program may use at most 64 MiB of HBM per device.

v0:
```python
import math

import jax
import jax.numpy as jnp
from jax import lax
from jax.sharding import PartitionSpec as P

very_low = -1e30


def copy_for_each(value, axis):
    count = lax.axis_size(axis)
    return lax.all_to_all(
        jnp.broadcast_to(value[None], (count, *value.shape)), axis, 0, 0, tiled=True
    )


def in_order(pieces, dim):
    pieces = jnp.moveaxis(pieces, 0, dim)
    lengths = pieces.shape
    return pieces.reshape(*lengths[:dim], lengths[dim] * lengths[dim + 1], *lengths[dim + 2 :])


def collect(value, axis, dim):
    pieces = copy_for_each(value, axis)
    return in_order(pieces, dim)


def sent_together(arrays, axis, split_dim, concat_dim, along):
    columns = [a.reshape(*a.shape[:along], -1) for a in arrays]
    both = jnp.concatenate(columns, axis=along)
    result, at, outs = (
        lax.all_to_all(both, axis, split_axis=split_dim, concat_axis=concat_dim, tiled=True),
        0,
        [],
    )
    for a, column in zip(arrays, columns):
        share = result[..., at : at + column.shape[along]]
        outs.append(share.reshape(*share.shape[:along], *a.shape[along:]))
        at += column.shape[along]
    return tuple(outs)


def of_everyone(value, axis):
    everything = copy_for_each(value, axis)
    return jnp.sum(everything.astype(jnp.float32), axis=0)


def cut_along(value, dim, count):
    lengths = value.shape
    pieces = value.reshape(*lengths[:dim], count, lengths[dim] // count, *lengths[dim + 1 :])
    return jnp.moveaxis(pieces, dim, 0)


def summed_on_arrival(value, axis, dim):
    pieces = cut_along(value, dim, lax.axis_size(axis))
    arrived = lax.all_to_all(pieces, axis, split_axis=0, concat_axis=0, tiled=True)
    return arrived.astype(jnp.float32).sum(axis=0)


def masked_top(scores, allowed):
    return jnp.max(jnp.where(allowed, scores, very_low), axis=-1)


def spread_weights(scores, allowed, row_top):
    return jnp.where(allowed, jnp.exp(scores - row_top[..., None]), 0.0)


def per_device(
    residual,
    queries,
    kv_cache,
    kv_pages,
    cache_len,
    page_row,
    page_len,
    routes,
    route_weight,
    out_weight,
    gate_weight,
    up_weight,
    down_weight,
):
    pool_size = lax.axis_size("pool")
    expert_size = lax.axis_size("expert")
    pool_index = lax.axis_index("pool")
    rows_here, step_count, heads_here, head_dim = queries.shape
    kv_heads = kv_cache.shape[2]
    page_size = kv_pages.shape[2]
    model_width = residual.shape[2]
    score_scale = 1.0 / math.sqrt(head_dim)
    group_head = pool_index * kv_heads // pool_size
    own_cache = lax.dynamic_index_in_dim(kv_cache, group_head, 2, keepdims=False)
    cache_keys = own_cache[:, :, 0]
    cache_values = own_cache[:, :, 1]
    last_seen = cache_len[:, None] + jnp.arange(step_count, dtype=jnp.int32)[None, :]
    cache_valid = (
        jnp.arange(kv_cache.shape[1], dtype=jnp.int32)[None, None, :] <= last_seen[:, :, None]
    )[:, :, None, :]
    cache_scores = (
        jnp.einsum("rthd,rld->rthl", queries, cache_keys, preferred_element_type=jnp.float32)
        * score_scale
    )
    row_ids = jnp.arange(rows_here, dtype=jnp.int32)
    token_ids = jnp.arange(page_size, dtype=jnp.int32)
    owner_rows = page_row[:, 0]
    owner_sizes = page_len[:, 0]
    every_query = collect(queries, "pool", 2)
    all_heads = every_query.shape[2]
    grouped = every_query.reshape(rows_here, step_count, kv_heads, all_heads // kv_heads, head_dim)
    local_pages = kv_pages[:, 0]
    page_count = local_pages.shape[0]
    page_keys = local_pages[:, :, :, 0].reshape(page_count * page_size, kv_heads, head_dim)
    page_values = local_pages[:, :, :, 1].reshape(page_count * page_size, kv_heads, head_dim)
    local_rows = lax.dynamic_slice_in_dim(owner_rows, pool_index * page_count, page_count)
    local_sizes = lax.dynamic_slice_in_dim(owner_sizes, pool_index * page_count, page_count)
    page_valid = (local_rows[None, :, None] == row_ids[:, None, None]) & (
        token_ids[None, :] < local_sizes[:, None]
    )[None]
    page_valid = page_valid.reshape(rows_here, 1, 1, 1, -1)
    page_scores = (
        jnp.einsum("rtgjd,kgd->rtgjk", grouped, page_keys, preferred_element_type=jnp.float32)
        * score_scale
    )
    page_top = masked_top(page_scores, page_valid)
    page_weights = spread_weights(page_scores, page_valid, page_top)
    page_mixed = jnp.einsum(
        "rtgjk,kgd->rtgjd",
        page_weights.astype(jnp.bfloat16),
        page_values,
        preferred_element_type=jnp.float32,
    )
    head_shape = (1, rows_here, step_count, all_heads)
    mixed_parts, top_parts, total_parts = tuple(
        (
            part.astype(jnp.float32)
            for part in sent_together(
                (
                    page_mixed.reshape(head_shape + (head_dim,)).astype(jnp.bfloat16),
                    page_top.reshape(head_shape).astype(jnp.bfloat16),
                    jnp.sum(page_weights, axis=-1).reshape(head_shape).astype(jnp.bfloat16),
                ),
                "pool",
                3,
                0,
                4,
            )
        )
    )
    own_top = masked_top(cache_scores, cache_valid)
    own_weights = spread_weights(cache_scores, cache_valid, own_top)
    own_total = jnp.sum(own_weights, axis=-1)
    own_mixed = jnp.einsum(
        "rthl,rld->rthd",
        own_weights.astype(jnp.bfloat16),
        cache_values,
        preferred_element_type=jnp.float32,
    )
    row_top = jnp.maximum(own_top, jnp.max(top_parts, axis=0))
    own_factor = jnp.exp(own_top - row_top)
    part_factor = jnp.exp(top_parts - row_top[None])
    numerator = own_mixed * own_factor[..., None] + jnp.sum(
        mixed_parts * part_factor[..., None], axis=0
    )
    denominator = own_total * own_factor + jnp.sum(total_parts * part_factor, axis=0)
    attended = numerator / denominator[..., None]
    tokens_here = rows_here * step_count
    attended_low = attended.astype(jnp.bfloat16).reshape(tokens_here, heads_here * head_dim)
    projected = jnp.dot(attended_low, out_weight, preferred_element_type=jnp.float32)
    projected = of_everyone(projected.astype(jnp.bfloat16), "pool").astype(jnp.float32)
    hidden = residual.reshape(tokens_here, model_width).astype(jnp.float32) + projected
    hidden_low = hidden.astype(jnp.bfloat16)
    local_experts = gate_weight.shape[0]
    experts = local_experts * expert_size
    top_count = routes.shape[2]
    capacity = max(2, (3 * rows_here * top_count + experts - 1) // experts)
    flat_routes = routes.reshape(tokens_here * top_count)
    pick_table = (flat_routes[:, None] == jnp.arange(experts, dtype=jnp.int32)[None, :]).astype(
        jnp.int32
    )
    slot_index = jnp.sum((jnp.cumsum(pick_table, axis=0) - 1) * pick_table, axis=1)
    position = flat_routes * capacity + slot_index
    token_position = position.reshape(tokens_here, top_count)
    slot_ids = jnp.arange(experts * capacity, dtype=jnp.int32)
    select_tokens = jnp.sum(
        (token_position[:, :, None] == slot_ids[None, None, :]).astype(jnp.int32), axis=1
    ).astype(jnp.bfloat16)
    column_count = model_width // pool_size
    own_columns = lax.dynamic_slice_in_dim(hidden_low, pool_index * column_count, column_count, 1)
    outgoing_part = jnp.einsum(
        "tc,td->cd", select_tokens, own_columns, preferred_element_type=jnp.float32
    ).astype(jnp.bfloat16)
    arrived_part = lax.all_to_all(outgoing_part, "expert", split_axis=0, concat_axis=0, tiled=True)
    arrived_rows = collect(arrived_part, "pool", 1)
    batched = arrived_rows.reshape(expert_size, local_experts, capacity, model_width)
    gate_value = jnp.einsum(
        "sjcd,jdf->sjcf", batched, gate_weight, preferred_element_type=jnp.float32
    )
    upward = jnp.einsum("sjcd,jdf->sjcf", batched, up_weight, preferred_element_type=jnp.float32)
    active = (jax.nn.silu(gate_value) * upward).astype(jnp.bfloat16)
    partial_value = jnp.einsum(
        "sjcf,jfd->sjcd", active, down_weight, preferred_element_type=jnp.float32
    ).astype(jnp.bfloat16)
    partial_value = partial_value.reshape(experts * capacity, model_width)
    pair_weights = route_weight.reshape(tokens_here, top_count)
    shares = summed_on_arrival(partial_value.astype(jnp.float32).astype(jnp.bfloat16), "pool", 1)
    returned = lax.all_to_all(
        shares.astype(jnp.bfloat16), "expert", split_axis=0, concat_axis=0, tiled=True
    ).astype(shares.dtype)
    picked = jnp.take(returned, position, axis=0).reshape(tokens_here, top_count, column_count)
    weighted = jnp.sum(pair_weights[..., None] * picked, axis=1)
    expert_sum = collect(weighted.astype(jnp.bfloat16), "pool", 1).astype(weighted.dtype)
    output = (hidden + expert_sum).astype(jnp.bfloat16).reshape(rows_here, step_count, model_width)
    return output


def solution(mesh):
    return jax.shard_map(
        per_device,
        mesh=mesh,
        in_specs=(
            P("expert", None, None),
            P("expert", None, "pool", None),
            P("expert", None, None, None, None),
            P("pool", "expert", None, None, None, None),
            P("expert"),
            P(None, "expert"),
            P(None, "expert"),
            P("expert", None, None),
            P("expert", None, None),
            P("pool", None),
            P("expert", None, "pool"),
            P("expert", None, "pool"),
            P("expert", "pool", None),
        ),
        out_specs=P("expert", None, None),
        check_vma=False,
    )
```

profile of v0, /device:TPU:1, one launch (start us, length us, event | category | flops | bytes accessed | tf_op | source)
XLA Modules:
  0.0 195.9 jit_solution(8011467330210198432)
XLA Ops:
  1.5 6.5 %all-to-all-start = ((bf16[8,8,2,4,128]{4,1,3,2,0:T(8,128)(2,1)}), bf16[8,8,2,4,128]{4,1,3,2,0:T(8,128)(2,1)S(1)}, u32[]{:S(2)}, u32[]{:S(2)}) async-start(bf16[8,8,2,4,128]{4,1,3,2,0:T(8,128)(2,1)} %broadcast_in_dim.94), calls=%async_computation | async-start | bytes 262144 | tf_op jit(solution)/shard_map/all_to_all | solution.py:13
  10.8 3.0 %constant_dynamic-slice_fusion.2 = bf16[8,512,1,2,128]{4,3,2,1,0:T(2,128)(2,1)S(1)} fusion(bf16[8,512,2,2,128]{4,3,2,1,0:T(2,128)(2,1)} %param.15, s32[]{:T(128)S(6)} %select_n.53), kind=kLoop, calls=%fused_computation.93 | loop fusion | bytes 4194308 | tf_op jit(solution)/shard_map/jit(dynamic_index_in_dim)/dynamic_slice | solution.py:93
  18.8 4.8 %all-to-all-start.1 = ((bf16[1,8,2,32,130]{4,2,1,0,3:T(2,128)(2,1)}), bf16[1,8,2,32,130]{4,2,1,0,3:T(2,128)(2,1)S(1)}, u32[]{:S(2)}, u32[]{:S(2)}) async-start(bf16[1,8,2,32,130]{4,2,1,0,3:T(2,128)(2,1)} %copy.181), calls=%async_computation.1 | async-start | bytes 524288 | tf_op jit(solution)/shard_map/all_to_all | solution.py:33
  24.0 6.2 %all-to-all-done.1 = bf16[1,8,2,32,130]{4,2,1,0,3:T(2,128)(2,1)S(1)} async-done(((bf16[1,8,2,32,130]{4,2,1,0,3:T(2,128)(2,1)}), bf16[1,8,2,32,130]{4,2,1,0,3:T(2,128)(2,1)S(1)}, u32[]{:S(2)}, u32[]{:S(2)}) %all-to-all-start.1) | async-done | bytes 133152 | tf_op jit(solution)/shard_map/all_to_all | solution.py:33
  30.1 2.9 %copy.183 = bf16[1,8,2,8,4,130]{1,3,5,4,2,0:T(8,128)(2,1)} copy(bf16[1,8,2,8,4,130]{5,2,1,4,3,0:T(2,128)(2,1)S(1)} %bitcast.146) | data formatting | bytes 266240 | tf_op jit(solution)/shard_map/all_to_all | solution.py:33
  35.5 3.0 %multiply_reduce_fusion = f32[8,2,4,128]{0,3,2,1:T(8,128)S(1)} fusion(bf16[8,8,2,4,130]{1,0,4,3,2:T(8,128)(2,1)} %bitcast.141, f32[8,8,2,4]{1,0,3,2:T(8,128)S(1)} %fusion.55), kind=kLoop, calls=%fused_computation.4 | loop fusion | flops 188416 | bytes 165888 | tf_op jit(solution)/shard_map/reduce_sum | solution.py:162
  40.3 2.8 %convolution_convert_fusion.1 = bf16[16,4096]{1,0:T(8,128)(2,1)S(1)} fusion(bf16[512,4096]{1,0:T(8,128)(2,1)} %param.22, bf16[2,8,4,128]{3,2,1,0:T(4,128)(2,1)S(1)} %bitcast.159), kind=kOutput, calls=%fused_computation.3 | convolution fusion | flops 67174400 | bytes 4341760 | tf_op jit(solution)/shard_map/dot_general | solution.py:169
  44.2 4.5 %all-to-all-start.2 = ((bf16[8,16,4096]{2,1,0:T(8,128)(2,1)}), bf16[8,16,4096]{2,1,0:T(8,128)(2,1)S(1)}, u32[]{:S(2)}, u32[]{:S(2)}) async-start(bf16[8,16,4096]{2,1,0:T(8,128)(2,1)} %broadcast_in_dim.97), calls=%async_computation.2 | async-start | bytes 2097152 | tf_op jit(solution)/shard_map/all_to_all | solution.py:13
  50.8 12.9 %all-to-all-done.2 = bf16[8,16,4096]{2,1,0:T(8,128)(2,1)S(1)} async-done(((bf16[8,16,4096]{2,1,0:T(8,128)(2,1)}), bf16[8,16,4096]{2,1,0:T(8,128)(2,1)S(1)}, u32[]{:S(2)}, u32[]{:S(2)}) %all-to-all-start.2) | async-done | bytes 1048608 | tf_op jit(solution)/shard_map/all_to_all | solution.py:13
  64.9 20.0 %all_to_all.61 = bf16[32,6,512]{2,1,0:T(8,128)(2,1)S(1)} all-to-all(bf16[32,6,512]{2,1,0:T(8,128)(2,1)S(1)} %all_to_all.46), channel_id=1, replica_groups=mesh['pool'=8,'expert'=32] {'expert'}, dimensions={0} | all-to-all | bytes 393216 | tf_op jit(solution)/shard_map/all_to_all | solution.py:193
  85.1 26.7 %all_to_all.62 = bf16[8,192,512]{2,1,0:T(8,128)(2,1)S(1)} all-to-all(bf16[8,192,512]{2,1,0:T(8,128)(2,1)S(1)} %broadcast_in_dim.100), channel_id=1, replica_groups=mesh['pool'=8,'expert'=32] {'pool'}, dimensions={0} | all-to-all | bytes 3145728 | tf_op jit(solution)/shard_map/all_to_all | solution.py:13
  111.8 2.0 %copy.192 = bf16[192,8,512]{2,1,0:T(8,128)(2,1)} copy(bf16[192,8,512]{2,0,1:T(8,128)(2,1)S(1)} %bitcast.142) | data formatting | bytes 3145728 | tf_op jit(solution)/shard_map/transpose | solution.py:19
  113.8 5.6 %reshape_reshape.7 = bf16[32,2,3,4096]{3,2,1,0:T(4,128)(2,1)} reshape(bf16[192,8,512]{2,1,0:T(8,128)(2,1)} %copy.192) | data formatting | bytes 3145728 | tf_op jit(solution)/shard_map/reshape;reshape | solution.py:195
  119.3 3.7 %fusion.9 = f32[32,2,3,128]{3,0,2,1:T(8,128)S(1)} fusion(bf16[2,4096,128]{2,1,0:T(8,128)(2,1)} %param.23, bf16[32,2,3,4096]{3,2,1,0:T(4,128)(2,1)} %reshape_reshape.7), kind=kOutput, calls=%fused_computation.19 | convolution fusion | flops 201326592 | bytes 3768320 | tf_op jit(solution)/shard_map/sjcd,jdf->sjcf/dot_general | solution.py:196
  123.0 5.3 %fusion = bf16[32,2,3,4096]{3,0,2,1:T(8,128)(2,1)} fusion(bf16[2,128,4096]{2,1,0:T(8,128)(2,1)S(1)} %copy-done, bf16[2,4096,128]{2,1,0:T(8,128)(2,1)} %param.24, bf16[32,2,3,4096]{3,2,1,0:T(4,128)(2,1)} %reshape_reshape.7, f32[32,2,3,128]{3,0,2,1:T(8,128)S(1)} %fusion.9), kind=kOutput, calls=%fused_computation.2 | convolution fusion | flops 403587072 | bytes 7438336 | tf_op jit(solution)/shard_map/sjcf,jfd->sjcd/dot_general | solution.py:201
  128.3 4.1 %copy.195 = bf16[32,2,3,4096]{3,2,1,0:T(4,128)(2,1)} copy(bf16[32,2,3,4096]{3,0,2,1:T(8,128)(2,1)} %fusion) | data formatting | bytes 3145728 | tf_op jit(solution)/shard_map/convert_element_type | solution.py:203
  132.4 5.4 %reshape.257 = bf16[192,8,512]{2,1,0:T(8,128)(2,1)} reshape(bf16[32,2,3,4096]{3,2,1,0:T(4,128)(2,1)} %copy.195) | data formatting | bytes 3145728 | tf_op jit(solution)/shard_map/reshape | solution.py:51
  137.8 1.9 copy.196
  139.7 24.7 %all_to_all.63 = bf16[8,192,512]{2,1,0:T(8,128)(2,1)} all-to-all(bf16[8,192,512]{2,1,0:T(8,128)(2,1)S(1)} %copy.196), channel_id=1, replica_groups=mesh['pool'=8,'expert'=32] {'pool'}, dimensions={0} | all-to-all | bytes 3145728 | tf_op jit(solution)/shard_map/all_to_all | solution.py:57
  164.4 1.7 reduce_sum.99
  166.9 4.2 %all-to-all-start.6 = ((bf16[32,6,512]{2,1,0:T(8,128)(2,1)}), bf16[32,6,512]{2,1,0:T(8,128)(2,1)S(1)}, u32[]{:S(2)}, u32[]{:S(2)}) async-start(bf16[32,6,512]{2,1,0:T(8,128)(2,1)} %all_to_all.50), calls=%async_computation.6 | async-start | bytes 524288 | tf_op jit(solution)/shard_map/all_to_all | solution.py:207
  171.2 9.5 %all-to-all-done.6 = bf16[32,6,512]{2,1,0:T(8,128)(2,1)S(1)} async-done(((bf16[32,6,512]{2,1,0:T(8,128)(2,1)}), bf16[32,6,512]{2,1,0:T(8,128)(2,1)S(1)}, u32[]{:S(2)}, u32[]{:S(2)}) %all-to-all-start.6) | async-done | bytes 196640 | tf_op jit(solution)/shard_map/all_to_all | solution.py:207
  182.4 6.9 %all-to-all-start.7 = ((bf16[8,16,512]{2,1,0:T(8,128)(2,1)}), bf16[8,16,512]{2,1,0:T(8,128)(2,1)S(1)}, u32[]{:S(2)}, u32[]{:S(2)}) async-start(bf16[8,16,512]{2,1,0:T(8,128)(2,1)} %broadcast_in_dim.102), calls=%async_computation.7 | async-start | bytes 262144 | tf_op jit(solution)/shard_map/all_to_all | solution.py:13
  189.5 5.1 %all-to-all-done.7 = bf16[8,16,512]{2,1,0:T(8,128)(2,1)S(1)} async-done(((bf16[8,16,512]{2,1,0:T(8,128)(2,1)}), bf16[8,16,512]{2,1,0:T(8,128)(2,1)S(1)}, u32[]{:S(2)}, u32[]{:S(2)}) %all-to-all-start.7) | async-done | bytes 131104 | tf_op jit(solution)/shard_map/all_to_all | solution.py:13
  (86 shorter events, 22.2 us)
Async XLA Ops:
  0.0 123.0 %copy-start = (bf16[2,128,4096]{2,1,0:T(8,128)(2,1)S(1)}, bf16[2,128,4096]{2,1,0:T(8,128)(2,1)}, u32[]{:S(2)}) copy-start(bf16[2,128,4096]{2,1,0:T(8,128)(2,1)} %param.25) | copy-start | bytes 6291460
  1.5 14.8 %all-to-all-start = ((bf16[8,8,2,4,128]{4,1,3,2,0:T(8,128)(2,1)}), bf16[8,8,2,4,128]{4,1,3,2,0:T(8,128)(2,1)S(1)}, u32[]{:S(2)}, u32[]{:S(2)}) async-start(bf16[8,8,2,4,128]{4,1,3,2,0:T(8,128)(2,1)} %broadcast_in_dim.94), calls=%async_computation | async-start | bytes 262144 | tf_op jit(solution)/shard_map/all_to_all | solution.py:13
  13.8 0.7 copy-start.6
  13.8 2.0 copy-start.4
  14.5 1.3 copy-start.1
  18.8 11.3 %all-to-all-start.1 = ((bf16[1,8,2,32,130]{4,2,1,0,3:T(2,128)(2,1)}), bf16[1,8,2,32,130]{4,2,1,0,3:T(2,128)(2,1)S(1)}, u32[]{:S(2)}, u32[]{:S(2)}) async-start(bf16[1,8,2,32,130]{4,2,1,0,3:T(2,128)(2,1)} %copy.181), calls=%async_computation.1 | async-start | bytes 524288 | tf_op jit(solution)/shard_map/all_to_all | solution.py:33
  43.1 5.6 %copy-start.3 = (s32[8,2,8]{2,1,0:T(2,128)S(1)}, s32[8,2,8]{2,1,0:T(2,128)}, u32[]{:S(2)}) copy-start(s32[8,2,8]{2,1,0:T(2,128)} %param.20) | copy-start | bytes 1540
  43.1 6.2 %copy-start.2 = (bf16[8,2,4096]{2,1,0:T(2,128)(2,1)S(1)}, bf16[8,2,4096]{2,1,0:T(2,128)(2,1)}, u32[]{:S(2)}) copy-start(bf16[8,2,4096]{2,1,0:T(2,128)(2,1)} %param.13) | copy-start | bytes 393220
  44.2 19.5 %all-to-all-start.2 = ((bf16[8,16,4096]{2,1,0:T(8,128)(2,1)}), bf16[8,16,4096]{2,1,0:T(8,128)(2,1)S(1)}, u32[]{:S(2)}, u32[]{:S(2)}) async-start(bf16[8,16,4096]{2,1,0:T(8,128)(2,1)} %broadcast_in_dim.97), calls=%async_computation.2 | async-start | bytes 2097152 | tf_op jit(solution)/shard_map/all_to_all | solution.py:13
  166.1 15.5 %copy-start.5 = (f32[8,2,8]{2,1,0:T(2,128)S(1)}, f32[8,2,8]{2,1,0:T(2,128)}, u32[]{:S(2)}) copy-start(f32[8,2,8]{2,1,0:T(2,128)} %param.21) | copy-start | bytes 1540
  166.9 13.9 %all-to-all-start.6 = ((bf16[32,6,512]{2,1,0:T(8,128)(2,1)}), bf16[32,6,512]{2,1,0:T(8,128)(2,1)S(1)}, u32[]{:S(2)}, u32[]{:S(2)}) async-start(bf16[32,6,512]{2,1,0:T(8,128)(2,1)} %all_to_all.50), calls=%async_computation.6 | async-start | bytes 524288 | tf_op jit(solution)/shard_map/all_to_all | solution.py:207
  182.4 12.2 %all-to-all-start.7 = ((bf16[8,16,512]{2,1,0:T(8,128)(2,1)}), bf16[8,16,512]{2,1,0:T(8,128)(2,1)S(1)}, u32[]{:S(2)}, u32[]{:S(2)}) async-start(bf16[8,16,512]{2,1,0:T(8,128)(2,1)} %broadcast_in_dim.102), calls=%async_computation.7 | async-start | bytes 262144 | tf_op jit(solution)/shard_map/all_to_all | solution.py:13
where the time goes:
time: 197 us; the launch traced here: 196 us
  blocking collectives  71.3 us (36%)
  local copies, waits for them, and re-layouts  38 us (19%)
  waiting for transfers between devices  33.7 us (17%)
  starting transfers between devices  26.9 us (14%)
  matrix products  15.5 us (8%)
  other arithmetic  10.1 us (5%)
    all_to_all x1, blocking collectives, copy_for_each(): lax.all_to_all(jnp.broadcast_to(value[None], (count, *value.shape)), axis...  26.7 us
    all_to_all x1, blocking collectives, summed_on_arrival(): lax.all_to_all(pieces, axis, split_axis=0, concat_axis=0, tiled=True)  24.7 us
    all_to_all x1, blocking collectives, per_device(): lax.all_to_all(outgoing_part, 'expert', split_axis=0, concat_axis=0, tile...  20 us
    all_to_all x3, waiting for transfers between devices, copy_for_each(): lax.all_to_all(jnp.broadcast_to(value[None], (count, *value.shape)), axis...  18 us
    all_to_all x3, starting transfers between devices, copy_for_each(): lax.all_to_all(jnp.broadcast_to(value[None], (count, *value.shape)), axis...  17.9 us
    all_to_all x1, waiting for transfers between devices, per_device(): lax.all_to_all(shares.astype(jnp.bfloat16), 'expert', split_axis=0, conca...  9.53 us
    all_to_all x1, waiting for transfers between devices, sent_together(): lax.all_to_all(both, axis, split_axis=split_dim, concat_axis=concat_dim,...  6.16 us
    another operation x1, local copies, waits for them, and re-layouts, per_device(): arrived_rows.reshape(expert_size, local_experts, capacity, model_width)  5.56 us
  transfers between devices with their start and end apart: 5, of which 4 were waited for; matrix products, arithmetic and copies ran while one was open for 5% of the time, Pallas kernels for 0%

commit v1 on v0

v1 whole, which is shorter than its diff:
```python
import functools
import math

import jax
import jax.numpy as jnp
from jax import lax
from jax.experimental import pallas as pl
from jax.experimental.pallas import tpu as pltpu
from jax.sharding import PartitionSpec as P

very_low = -1e30
MESH = pl.DeviceIdType.MESH
bf16, f32 = jnp.bfloat16, jnp.float32
POOL, EXPERT = 8, 32
CAP = 3
NCH = 2
ROWS = EXPERT * 2 * CAP
CR = ROWS // NCH
CO = EXPERT // NCH
PAIR = 2 * CAP


def local_copy(src, dst, sem):
    return pltpu.make_async_copy(src, dst, sem)


def remote(src, dst, ssem, rsem, **where):
    return pltpu.make_async_remote_copy(
        src_ref=src, dst_ref=dst, send_sem=ssem, recv_sem=rsem, device_id=where, device_id_type=MESH
    )


def wait_bytes(ref, sem):
    pltpu.make_async_copy(ref, ref, sem).wait()


def offset_of(o):
    dzi, dx = o // 4, o % 4
    return dx, ((dzi + 1) // 2) * (2 * (dzi % 2) - 1)


def dot_t(a, b):
    return lax.dot_general(a, b, (((1,), (1,)), ((), ())), preferred_element_type=f32)


def dot(a, b):
    return jnp.dot(a, b, preferred_element_type=f32)


def layer_kernel(
    clen, prow, plen, res, q, routes, rw, kv, pages, ow, gw, uw, dw,
    out,
    kvb, pgb, owb, gwb, uwb, dwb, resb,
    qall, psnd, prcv, own_m, own_top, own_tot, row_top, att,
    osnd, orcv, hid, selw, dsnd, xg, acc, act,
    xsnd, xrcv, part, ssnd, rrcv, fin, rsnd, ret, fsnd, fall,
    lsem, kvsem, qs, qr, ps, pr, os_, or_, ds_, dr, as_, ar, fs, fr,
    xs, xr, rs, rr, ts, tr, es, er,
):
    p = lax.axis_index("pool")
    e = lax.axis_index("expert")
    y, c = p // 2, p % 2
    ex, ez = e // 8, e % 8
    partner = y * 2 + (1 - c)
    head = p // 4
    scale = 1.0 / math.sqrt(128)

    barrier = pltpu.get_barrier_semaphore()

    def greet_pool(k, carry):
        pl.semaphore_signal(barrier, inc=1, device_id={"pool": (p + k) % POOL}, device_id_type=MESH)
        return carry

    def greet_expert(k, carry):
        pl.semaphore_signal(barrier, inc=1, device_id={"expert": (e + k) % EXPERT}, device_id_type=MESH)
        return carry

    lax.fori_loop(1, EXPERT, greet_expert, 0)
    lax.fori_loop(1, POOL, greet_pool, 0)

    for r in range(8):
        local_copy(kv.at[r, :, head], kvb.at[r], kvsem.at[r]).start()
    local_copy(pages.at[:, 0, :, 0], pgb.at[0], lsem.at[0]).start()
    local_copy(pages.at[:, 0, :, 1], pgb.at[1], lsem.at[1]).start()
    own_cols = pl.ds(pl.multiple_of(p * 512, 512), 512)
    local_copy(res.at[:, :, own_cols], resb, lsem.at[2]).start()
    local_copy(ow, owb, lsem.at[3]).start()
    local_copy(gw, gwb, lsem.at[4]).start()
    local_copy(uw, uwb, lsem.at[5]).start()
    local_copy(dw, dwb, lsem.at[6]).start()
    local_copy(q, qall.at[p], qr).start()

    lane = lax.broadcasted_iota(jnp.int32, (16, ROWS), 1).astype(f32)
    spot = jnp.floor((lane + 0.5) * (1.0 / PAIR))
    within = lane - spot * PAIR
    which = jnp.where(within >= CAP, 1.0, 0.0)
    slot = within - which * CAP
    dzi = jnp.floor((spot + 0.5) * 0.25)
    dx = spot - dzi * 4
    half = jnp.floor((dzi + 1.5) * 0.5)
    odd = dzi - 2.0 * jnp.floor((dzi + 0.5) * 0.5)
    dz = half * (2.0 * odd - 1.0)
    gx = ex.astype(f32) - dx
    gx = jnp.where(gx < 0, gx + 4, gx)
    gz = ez.astype(f32) - dz
    gz = jnp.where(gz < 0, gz + 8, jnp.where(gz >= 8, gz - 8, gz))
    expert_id = (gx * 8 + gz) * 2 + which
    names = routes[...].reshape(16, 8).astype(f32)
    strengths = rw[...].reshape(16, 8)
    chosen = jnp.zeros((16, ROWS), f32)
    strength = jnp.zeros((16, ROWS), f32)
    for k in range(8):
        hit = names[:, k : k + 1] == expert_id
        chosen = jnp.where(hit, 1.0, chosen)
        strength = jnp.where(hit, strengths[:, k : k + 1], strength)
    earlier = (
        lax.broadcasted_iota(jnp.int32, (16, 16), 1) < lax.broadcasted_iota(jnp.int32, (16, 16), 0)
    ).astype(f32).astype(bf16)
    before = dot(earlier, chosen.astype(bf16))
    taken = jnp.where(before == slot, chosen, 0.0)
    selw[0] = taken
    selw[1] = taken * strength

    def cache_row(r):
        keys = kvb.reshape(8, 1024, 128)[r]
        s = dot_t(q[r].reshape(8, 128), keys) * scale
        col = lax.broadcasted_iota(jnp.int32, (8, 1024), 1)
        step = lax.broadcasted_iota(jnp.int32, (8, 1024), 0) // 4
        seen = (col % 2 == 0) & (col <= 2 * (clen[r] + step))
        top = jnp.max(jnp.where(seen, s, very_low), axis=1, keepdims=True)
        w = jnp.where(seen, jnp.exp(s - top), 0.0)
        own_top[r] = jnp.broadcast_to(top, (8, 128))
        own_tot[r] = jnp.broadcast_to(jnp.sum(w, axis=1, keepdims=True), (8, 128))
        own_m[r] = dot(pltpu.roll(w, 1, 1).astype(bf16), keys)

    for r in range(4):
        local_copy(kv.at[r, :, head], kvb.at[r], kvsem.at[r]).wait()
    for r in range(4):
        cache_row(r)

    pl.semaphore_wait(barrier, EXPERT - 1 + POOL - 1)

    def send_query(k, carry):
        remote(q, qall.at[p], qs, qr, pool=(p + k) % POOL).start()
        return carry

    lax.fori_loop(1, POOL, send_query, 0)

    for r in range(4, 8):
        local_copy(kv.at[r, :, head], kvb.at[r], kvsem.at[r]).wait()
    for r in range(4, 8):
        cache_row(r)

    local_copy(pages.at[:, 0, :, 0], pgb.at[0], lsem.at[0]).wait()
    local_copy(pages.at[:, 0, :, 1], pgb.at[1], lsem.at[1]).wait()
    wait_bytes(qall, qr)
    lane128 = lax.broadcasted_iota(jnp.int32, (32, 128), 1)
    for s_ in range(4):
        row = prow[p * 4 + s_]
        filled = plen[p * 4 + s_]
        for g in range(2):
            keys = pgb.reshape(2, 4, 128, 128)[g, s_]
            asked = jnp.concatenate([qall[4 * g + i, row].reshape(8, 128) for i in range(4)], axis=0)
            s = dot_t(asked, keys) * scale
            seen = (lane128 % 2 == 0) & (lane128 < 2 * filled)
            top = jnp.max(jnp.where(seen, s, very_low), axis=1, keepdims=True)
            top = top.astype(bf16).astype(f32)
            w = jnp.where(seen, jnp.exp(s - top), 0.0)
            total = jnp.sum(w, axis=1, keepdims=True)
            mixed = dot(pltpu.roll(w, 1, 1).astype(bf16), keys).astype(bf16)
            high = total.astype(bf16).astype(f32)
            stats = jnp.where(lane128 < 32, top, jnp.where(lane128 < 64, high, total - high)).astype(bf16)
            for i in range(4):
                psnd[4 * g + i, 0, s_ * 8 : s_ * 8 + 8] = mixed[i * 8 : i * 8 + 8]
                psnd[4 * g + i, 1, s_ * 8 : s_ * 8 + 8] = stats[i * 8 : i * 8 + 8]

    local_copy(psnd.at[p], prcv.at[p], pr).start()

    def send_parts(k, carry):
        to = (p + k) % POOL
        remote(psnd.at[to], prcv.at[p], ps, pr, pool=to).start()
        return carry

    lax.fori_loop(1, POOL, send_parts, 0)
    local_copy(ow, owb, lsem.at[3]).wait()
    local_copy(res.at[:, :, own_cols], resb, lsem.at[2]).wait()
    wait_bytes(prcv, pr)

    tops = [own_top[r] for r in range(8)]
    match = []
    for n in range(32):
        st = prcv[n // 4, 1, (n % 4) * 8 : (n % 4) * 8 + 8].astype(f32)
        top = jnp.broadcast_to(st[:, 0:1], (8, 128))
        row = prow[n]
        flags = [jnp.where(row == r, 1.0, 0.0) for r in range(8)]
        match.append(flags)
        for r in range(8):
            tops[r] = jnp.maximum(tops[r], top + (flags[r] - 1.0) * 2e30)
    for r in range(8):
        row_top[r] = tops[r]
    nums, dens = [], []
    for r in range(8):
        factor = jnp.exp(own_top[r] - tops[r])
        nums.append(own_m[r] * factor)
        dens.append(own_tot[r] * factor)
    for n in range(32):
        st = prcv[n // 4, 1, (n % 4) * 8 : (n % 4) * 8 + 8].astype(f32)
        top = jnp.broadcast_to(st[:, 0:1], (8, 128))
        total = jnp.broadcast_to(st[:, 32:33] + st[:, 64:65], (8, 128))
        factor = jnp.exp(top - row_top[prow[n]])
        mixed = prcv[n // 4, 0, (n % 4) * 8 : (n % 4) * 8 + 8].astype(f32) * factor
        total = total * factor
        for r in range(8):
            nums[r] = nums[r] + mixed * match[n][r]
            dens[r] = dens[r] + total * match[n][r]
    for r in range(8):
        att[r * 8 : r * 8 + 8] = nums[r] / dens[r]
    attended = jnp.concatenate(
        [att[pl.ds(h, 16, stride=4), :].astype(bf16) for h in range(4)], axis=1
    )

    def project(k):
        to = (p + k) % POOL
        return to, dot(attended, owb[:, pl.ds(pl.multiple_of(to * 512, 512), 512)])

    for k in (4, 3, 5, 2, 6, 1, 7):
        to, value = project(k)
        osnd[k - 1] = value.astype(bf16)
        remote(osnd.at[k - 1], orcv.at[k - 1], os_.at[k - 1], or_.at[k - 1], pool=to).start()
    _, hidden = project(0)
    hidden = hidden + resb[...].reshape(16, 512).astype(f32)
    for k in range(1, 8):
        remote(osnd.at[k - 1], orcv.at[k - 1], os_.at[k - 1], or_.at[k - 1], pool=p).wait_recv()
        hidden = hidden + orcv[k - 1].astype(f32)
    hid[...] = hidden

    leaving = lax.dot_general(
        selw[0].astype(bf16), hidden.astype(bf16), (((0,), (0,)), ((), ())), preferred_element_type=f32
    ).astype(bf16)
    for b in range(4):
        dsnd[b] = leaving[:, b * 128 : (b + 1) * 128]

    def rows_of(o):
        return pl.ds(pl.multiple_of(o * PAIR, 2), PAIR)

    def chunk_rows(ch):
        return pl.ds(ch * CR, CR)

    local_copy(dsnd.at[:, pl.ds(0, PAIR), :], xg.at[p, :, pl.ds(0, PAIR), :], dr.at[0]).start()
    for ch in range(NCH):

        def send_rows(o, carry):
            dx_, dz_ = offset_of(o)
            to = ((ex - dx_ + 4) % 4) * 8 + (ez - dz_ + 8) % 8
            remote(
                dsnd.at[:, rows_of(o), :], xg.at[p, :, rows_of(o), :], ds_.at[ch], dr.at[ch], expert=to
            ).start()
            return carry

        lax.fori_loop(max(1, ch * CO), (ch + 1) * CO, send_rows, 0)

    def share(dy, core):
        return ((y + dy) % 4) * 2 + core

    def block_of(s, ch):
        return xg.at[s, :, chunk_rows(ch), :]

    def give(ch, dy):
        to = share(dy, c)
        return remote(block_of(p, ch), block_of(p, ch), as_.at[ch, dy], ar.at[ch, dy], pool=to)

    def pass_on(ch, dy):
        s = share(dy, c)
        return remote(block_of(s, ch), block_of(s, ch), fs.at[ch, dy], fr.at[ch, dy], pool=partner)

    def upward(ch, s, first=False):
        rows = jnp.concatenate([xg[s, b, chunk_rows(ch), :] for b in range(4)], axis=1)
        at = pl.ds(pl.multiple_of(s * 512, 512), 512)
        for j in range(2):
            w = jnp.concatenate([gwb[j, at, :], uwb[j, at, :]], axis=1)
            value = dot(rows, w)
            if first:
                acc[ch, j] = value
            else:
                acc[ch, j] += value

    for ch in range(NCH):
        wait_bytes(block_of(p, ch), dr.at[ch])
        for dy in (1, 3, 2):
            give(ch, dy).start()
        pass_on(ch, 0).start()
        if ch == 0:
            local_copy(gw, gwb, lsem.at[4]).wait()
            local_copy(uw, uwb, lsem.at[5]).wait()
        upward(ch, p, True)

    local_copy(dw, dwb, lsem.at[6]).wait()

    def experts(ch):
        pass_on(ch, 0).wait_recv()
        upward(ch, partner)
        for dy in (1, 3, 2):
            give(ch, (4 - dy) % 4).wait_recv()
            pass_on(ch, dy).start()
            upward(ch, share(dy, c))
        for dy in (1, 3, 2):
            pass_on(ch, dy).wait_recv()
            upward(ch, share(dy, 1 - c))
        row = lax.broadcasted_iota(jnp.int32, (CR, 128), 0).astype(f32)
        within = row - jnp.floor((row + 0.5) * (1.0 / PAIR)) * PAIR
        parts = []
        for j in range(2):
            gate, up = acc[ch, j, :, 0:128], acc[ch, j, :, 128:256]
            value = gate / (1.0 + jnp.exp(-gate)) * up
            mine = (within >= CAP) if j else (within < CAP)
            parts.append(jnp.where(mine, value, 0.0).astype(bf16))
        act[...] = jnp.concatenate(parts, axis=1)

    def down(s):
        at = pl.ds(pl.multiple_of(s * 512, 512), 512)
        return dot(act[...], dwb.reshape(256, 4096)[:, at])

    def across(ch, dy):
        return remote(xsnd.at[ch, dy], xrcv.at[ch, dy], xs.at[ch, dy], xr.at[ch, dy], pool=partner)

    def home(ch, dy):
        return remote(ssnd.at[ch, dy - 1], rrcv.at[ch, dy - 1], rs.at[ch, dy - 1], rr.at[ch, dy - 1], pool=share(dy, c))

    def outward(ch):
        for dy in (2, 1, 3, 0):
            value = down(share(dy, 1 - c)).astype(bf16)
            for b in range(4):
                xsnd[ch, dy, b] = value[:, b * 128 : (b + 1) * 128]
            across(ch, dy).start()
        for dy in (2, 1, 3, 0):
            part[dy] = down(share(dy, c))
        for dy in (2, 1, 3, 0):
            across(ch, dy).wait_recv()
            for b in range(4):
                value = part[dy, :, b * 128 : (b + 1) * 128] + xrcv[ch, dy, b].astype(f32)
                if dy:
                    ssnd[ch, dy - 1, b] = value.astype(bf16)
                else:
                    fin[b, chunk_rows(ch), :] = value
            if dy:
                home(ch, dy).start()

    def back(ch):
        for dy in (1, 3, 2):
            home(ch, dy).wait_recv()
        for b in range(4):
            value = fin[b, chunk_rows(ch), :]
            for dy in (1, 2, 3):
                value = value + rrcv[ch, dy - 1, b].astype(f32)
            rsnd[b, chunk_rows(ch), :] = value.astype(bf16)
        if ch == 0:
            local_copy(rsnd.at[:, pl.ds(0, PAIR), :], ret.at[:, pl.ds(0, PAIR), :], tr.at[0]).start()

        def send_rows(o, carry):
            dx_, dz_ = offset_of(o)
            to = ((ex + dx_) % 4) * 8 + (ez + dz_ + 8) % 8
            remote(rsnd.at[:, rows_of(o), :], ret.at[:, rows_of(o), :], ts.at[ch], tr.at[ch], expert=to).start()
            return carry

        lax.fori_loop(max(1, ch * CO), (ch + 1) * CO, send_rows, 0)

    experts(0)
    outward(0)
    for ch in range(1, NCH):
        experts(ch)
        outward(ch)
        back(ch - 1)
    back(NCH - 1)

    for ch in range(NCH):
        wait_bytes(ret.at[:, chunk_rows(ch), :], tr.at[ch])
    high = selw[1].astype(bf16)
    low = (selw[1] - high.astype(f32)).astype(bf16)
    returned = jnp.concatenate([ret[b] for b in range(4)], axis=1)
    summed = dot(jnp.concatenate([high, low], axis=0), returned)
    fsnd[...] = (hid[...] + (summed[0:16] + summed[16:32])).astype(bf16)
    local_copy(fsnd, fall.at[p], er).start()

    def send_result(k, carry):
        remote(fsnd, fall.at[p], es, er, pool=(p + k) % POOL).start()
        return carry

    lax.fori_loop(1, POOL, send_result, 0)
    wait_bytes(fall, er)
    for s in range(POOL):
        out[:, :, s * 512 : (s + 1) * 512] = fall[s].reshape(8, 2, 512)

    wait_bytes(qall.at[pl.ds(0, POOL - 1)], qs)
    wait_bytes(psnd.at[pl.ds(0, POOL - 1)], ps)
    wait_bytes(fall.at[pl.ds(0, POOL - 1)], es)
    for k in range(1, 8):
        remote(osnd.at[k - 1], orcv.at[k - 1], os_.at[k - 1], or_.at[k - 1], pool=p).wait_send()
    for ch in range(NCH):
        sent = pl.ds(0, CR - PAIR if ch == 0 else CR)
        wait_bytes(dsnd.at[:, sent, :], ds_.at[ch])
        wait_bytes(rsnd.at[:, sent, :], ts.at[ch])
        for dy in range(4):
            if dy:
                give(ch, dy).wait_send()
                home(ch, dy).wait_send()
            pass_on(ch, dy).wait_send()
            across(ch, dy).wait_send()


def per_device(
    residual, queries, kv_cache, kv_pages, cache_len, page_row, page_len, routes, route_weight,
    out_weight, gate_weight, up_weight, down_weight,
):
    smem = pl.BlockSpec(memory_space=pltpu.SMEM)
    vmem = pl.BlockSpec(memory_space=pltpu.VMEM)
    anywhere = pl.BlockSpec(memory_space=pl.ANY)
    dma = pltpu.SemaphoreType.DMA
    V = pltpu.VMEM
    return pl.pallas_call(
        layer_kernel,
        name="layer",
        out_shape=jax.ShapeDtypeStruct(residual.shape, bf16),
        in_specs=[smem] * 3 + [anywhere] + [vmem] * 3 + [anywhere] * 6,
        out_specs=vmem,
        scratch_shapes=[
            V((8, 512, 2, 128), bf16),
            V((2, 4, 64, 2, 128), bf16),
            V((512, 4096), bf16),
            V((2, 4096, 128), bf16),
            V((2, 4096, 128), bf16),
            V((2, 128, 4096), bf16),
            V((8, 2, 512), bf16),
            V((8, 8, 2, 4, 128), bf16),
            V((8, 2, 32, 128), bf16),
            V((8, 2, 32, 128), bf16),
            V((8, 8, 128), f32),
            V((8, 8, 128), f32),
            V((8, 8, 128), f32),
            V((8, 8, 128), f32),
            V((64, 128), f32),
            V((7, 16, 512), bf16),
            V((7, 16, 512), bf16),
            V((16, 512), f32),
            V((2, 16, ROWS), f32),
            V((4, ROWS, 128), bf16),
            V((8, 4, ROWS, 128), bf16),
            V((NCH, 2, CR, 256), f32),
            V((CR, 256), bf16),
            V((NCH, 4, 4, CR, 128), bf16),
            V((NCH, 4, 4, CR, 128), bf16),
            V((4, CR, 512), f32),
            V((NCH, 3, 4, CR, 128), bf16),
            V((NCH, 3, 4, CR, 128), bf16),
            V((4, ROWS, 128), f32),
            V((4, ROWS, 128), bf16),
            V((4, ROWS, 128), bf16),
            V((16, 512), bf16),
            V((8, 16, 512), bf16),
            dma((7,)), dma((8,)), dma(()), dma(()), dma(()), dma(()), dma((7,)), dma((7,)),
            dma((NCH,)), dma((NCH,)), dma((NCH, 4)), dma((NCH, 4)), dma((NCH, 4)), dma((NCH, 4)),
            dma((NCH, 4)), dma((NCH, 4)), dma((NCH, 3)), dma((NCH, 3)), dma((NCH,)), dma((NCH,)),
            dma(()), dma(()),
        ],
        compiler_params=pltpu.CompilerParams(
            collective_id=0, has_side_effects=True, vmem_limit_bytes=60 * 1024 * 1024
        ),
    )(
        cache_len, page_row.reshape(32), page_len.reshape(32), residual, queries, routes, route_weight,
        kv_cache, kv_pages, out_weight, gate_weight, up_weight, down_weight,
    )


def solution(mesh):
    return jax.shard_map(
        per_device,
        mesh=mesh,
        in_specs=(
            P("expert", None, None),
            P("expert", None, "pool", None),
            P("expert", None, None, None, None),
            P("pool", "expert", None, None, None, None),
            P("expert"),
            P(None, "expert"),
            P(None, "expert"),
            P("expert", None, None),
            P("expert", None, None),
            P("pool", None),
            P("expert", None, "pool"),
            P("expert", None, "pool"),
            P("expert", "pool", None),
        ),
        out_specs=P("expert", None, None),
        check_vma=False,
    )
```

time: 197 us -> 68.5 us (0.35)
  blocking collectives: 71.3 us -> 0 us
  Pallas kernels: 0 us -> 66.7 us
  local copies, waits for them, and re-layouts: 38 us -> 1.65 us
  waiting for transfers between devices: 33.7 us -> 0 us
  starting transfers between devices: 26.9 us -> 0 us
  matrix products: 15.5 us -> 0 us
  other arithmetic: 10.1 us -> 0 us
    all_to_all x3 -> x0, blocking collectives: 71.3 us -> none  [the longest x1 26.7 us: copy_for_each(): lax.all_to_all(jnp.broadcast_to(value[None], (count, *value.shape)), axis...]
    pallas_call x0 -> x1, Pallas kernels: none -> 66.7 us  [per_device(): pl.pallas_call(layer_kernel, name='layer', out_shape=jax.ShapeDtypeStruct...]
    all_to_all x5 -> x0, waiting for transfers between devices: 33.7 us -> none  [the longest x3 18 us: copy_for_each(): lax.all_to_all(jnp.broadcast_to(value[None], (count, *value.shape)), axis...]
    all_to_all x5 -> x0, starting transfers between devices: 26.9 us -> none  [the longest x3 17.9 us: copy_for_each(): lax.all_to_all(jnp.broadcast_to(value[None], (count, *value.shape)), axis...]
    dot_general x8 -> x0, matrix products: 15.5 us -> none  [the longest x1 5.29 us: per_device(): jnp.einsum('sjcf,jfd->sjcd', active, down_weight, preferred_element_type=...]
    reduce_sum x9 -> x0, other arithmetic: 7.17 us -> none  [the longest x1 3.04 us: per_device(): jnp.sum(mixed_parts * part_factor[..., None], axis=0)]
    convert_element_type x10 -> x0, local copies, waits for them, and re-layouts: 5.69 us -> none  [the longest x1 4.11 us: per_device(): partial_value = jnp.einsum('sjcf,jfd->sjcd', active, down_weight, preferr...]
    another operation x1 -> x0, local copies, waits for them, and re-layouts: 5.56 us -> none  [per_device(): arrived_rows.reshape(expert_size, local_experts, capacity, model_width)]
  transfers between devices with their start and end apart: 5 -> 0, of which waited for: 4 -> 0; matrix products, arithmetic and copies ran while one was open for 5% -> 0% of each run, Pallas kernels for 0% -> 0%
where the time goes in v1:
time: 68.5 us; the launch traced here: 68.3 us
  Pallas kernels  66.7 us (97%)
  local copies, waits for them, and re-layouts  1.65 us (2%)
    pallas_call x1, Pallas kernels, per_device(): pl.pallas_call(layer_kernel, name='layer', out_shape=jax.ShapeDtypeStruct...  66.7 us
    unnamed x1, local copies, waits for them, and re-layouts  1.65 us

profile of v1, /device:TPU:1, one launch (start us, length us, event | category | flops | bytes accessed | tf_op | source)
XLA Modules:
  0.0 68.3 jit_solution(3617605902965293882)
XLA Ops:
  0.0 66.7 %layer.1 = bf16[8,2,4096]{2,1,0:T(2,128)(2,1)} custom-call(s32[8]{0:T(128)} %clen.1, s32[32]{0:T(128)} %bitcast.2, s32[32]{0:T(128)} %bitcast.3, bf16[8,2,4096]{2,1,0:T(2,128)(2,1)} %res.1, bf16[8,2,4,128]{3,2,1,0:T(4,128)(2,1)} %q.1, s32[8,2,8]{2,1,0:T(2,128)} %routes.1, f32[8,2,8]{2,1,0:T(2,128)} %rw.1, bf16[8,512,2,2,128]{4,3,2,1,0:T(2,128)(2,1)} %kv.1, ...), custom_call_target="tpu_custom_call" | custom-call | tf_op jit(solution)/shard_map/layer/pallas_call | solution.py:419
  66.7 1.7 %copy.15 = bf16[8,2,4096]{2,1,0:T(2,128)(2,1)} copy(bf16[8,2,4096]{2,1,0:T(2,128)(2,1)} %layer.1) | data formatting | bytes 262144

commit v2 on v1

--- a/solution.py
+++ b/solution.py
@@ -13,11 +13,13 @@
 bf16, f32 = jnp.bfloat16, jnp.float32
 POOL, EXPERT = 8, 32
 CAP = 3
-NCH = 2
+NCH = 4
+ROT = 2
 ROWS = EXPERT * 2 * CAP
 CR = ROWS // NCH
 CO = EXPERT // NCH
 PAIR = 2 * CAP
+SELF = (-ROT) % 8 * 4
 
 
 def local_copy(src, dst, sem):
@@ -35,7 +37,7 @@
 
 
 def offset_of(o):
-    dzi, dx = o // 4, o % 4
+    dzi, dx = (o // 4 + ROT) % 8, o % 4
     return dx, ((dzi + 1) // 2) * (2 * (dzi % 2) - 1)
 
 
@@ -52,7 +54,7 @@
     out,
     kvb, pgb, owb, gwb, uwb, dwb, resb,
     qall, psnd, prcv, own_m, own_top, own_tot, row_top, att,
-    osnd, orcv, hid, selw, dsnd, xg, acc, act,
+    osnd, orcv, hid, selw, picks, q8, dsnd, xg, acc, act,
     xsnd, xrcv, part, ssnd, rrcv, fin, rsnd, ret, fsnd, fall,
     lsem, kvsem, qs, qr, ps, pr, os_, or_, ds_, dr, as_, ar, fs, fr,
     xs, xr, rs, rr, ts, tr, es, er,
@@ -88,7 +90,6 @@
     local_copy(gw, gwb, lsem.at[4]).start()
     local_copy(uw, uwb, lsem.at[5]).start()
     local_copy(dw, dwb, lsem.at[6]).start()
-    local_copy(q, qall.at[p], qr).start()
 
     lane = lax.broadcasted_iota(jnp.int32, (16, ROWS), 1).astype(f32)
     spot = jnp.floor((lane + 0.5) * (1.0 / PAIR))
@@ -97,6 +98,8 @@
     slot = within - which * CAP
     dzi = jnp.floor((spot + 0.5) * 0.25)
     dx = spot - dzi * 4
+    dzi = dzi + ROT
+    dzi = jnp.where(dzi >= 8, dzi - 8, dzi)
     half = jnp.floor((dzi + 1.5) * 0.5)
     odd = dzi - 2.0 * jnp.floor((dzi + 0.5) * 0.5)
     dz = half * (2.0 * odd - 1.0)
@@ -118,12 +121,13 @@
     ).astype(f32).astype(bf16)
     before = dot(earlier, chosen.astype(bf16))
     taken = jnp.where(before == slot, chosen, 0.0)
-    selw[0] = taken
-    selw[1] = taken * strength
+    picks[...] = taken.T.astype(bf16)
+    selw[...] = taken * strength
+    q8[...] = q[...].reshape(8, 8, 128)
 
     def cache_row(r):
         keys = kvb.reshape(8, 1024, 128)[r]
-        s = dot_t(q[r].reshape(8, 128), keys) * scale
+        s = dot_t(q8[r], keys) * scale
         col = lax.broadcasted_iota(jnp.int32, (8, 1024), 1)
         step = lax.broadcasted_iota(jnp.int32, (8, 1024), 0) // 4
         seen = (col % 2 == 0) & (col <= 2 * (clen[r] + step))
@@ -141,10 +145,11 @@
     pl.semaphore_wait(barrier, EXPERT - 1 + POOL - 1)
 
     def send_query(k, carry):
-        remote(q, qall.at[p], qs, qr, pool=(p + k) % POOL).start()
+        remote(q8, qall.at[p], qs, qr, pool=(p + k) % POOL).start()
         return carry
 
     lax.fori_loop(1, POOL, send_query, 0)
+    local_copy(q8, qall.at[p], qr).start()
 
     for r in range(4, 8):
         local_copy(kv.at[r, :, head], kvb.at[r], kvsem.at[r]).wait()
@@ -154,25 +159,30 @@
     local_copy(pages.at[:, 0, :, 0], pgb.at[0], lsem.at[0]).wait()
     local_copy(pages.at[:, 0, :, 1], pgb.at[1], lsem.at[1]).wait()
     wait_bytes(qall, qr)
-    lane128 = lax.broadcasted_iota(jnp.int32, (32, 128), 1)
+    scores = []
     for s_ in range(4):
         row = prow[p * 4 + s_]
-        filled = plen[p * 4 + s_]
         for g in range(2):
-            keys = pgb.reshape(2, 4, 128, 128)[g, s_]
-            asked = jnp.concatenate([qall[4 * g + i, row].reshape(8, 128) for i in range(4)], axis=0)
-            s = dot_t(asked, keys) * scale
-            seen = (lane128 % 2 == 0) & (lane128 < 2 * filled)
-            top = jnp.max(jnp.where(seen, s, very_low), axis=1, keepdims=True)
-            top = top.astype(bf16).astype(f32)
-            w = jnp.where(seen, jnp.exp(s - top), 0.0)
-            total = jnp.sum(w, axis=1, keepdims=True)
-            mixed = dot(pltpu.roll(w, 1, 1).astype(bf16), keys).astype(bf16)
-            high = total.astype(bf16).astype(f32)
-            stats = jnp.where(lane128 < 32, top, jnp.where(lane128 < 64, high, total - high)).astype(bf16)
+            asked = jnp.concatenate([qall[4 * g + i, row] for i in range(4)], axis=0)
+            scores.append(dot_t(asked, pgb.reshape(2, 4, 128, 128)[g, s_]))
+    scores = jnp.concatenate(scores, axis=0) * scale
+    lane128 = lax.broadcasted_iota(jnp.int32, (256, 128), 1)
+    limit = jnp.concatenate([jnp.full((64, 128), 2 * plen[p * 4 + s_], jnp.int32) for s_ in range(4)], axis=0)
+    seen = (lane128 % 2 == 0) & (lane128 < limit)
+    top = jnp.max(jnp.where(seen, scores, very_low), axis=1, keepdims=True)
+    top = top.astype(bf16).astype(f32)
+    w = jnp.where(seen, jnp.exp(scores - top), 0.0)
+    total = jnp.sum(w, axis=1, keepdims=True)
+    w = pltpu.roll(w, 1, 1).astype(bf16)
+    high = total.astype(bf16).astype(f32)
+    stats = jnp.where(lane128 < 32, top, jnp.where(lane128 < 64, high, total - high))
+    for s_ in range(4):
+        for g in range(2):
+            at = (s_ * 2 + g) * 32
+            mixed = dot(w[at : at + 32], pgb.reshape(2, 4, 128, 128)[g, s_])
             for i in range(4):
-                psnd[4 * g + i, 0, s_ * 8 : s_ * 8 + 8] = mixed[i * 8 : i * 8 + 8]
-                psnd[4 * g + i, 1, s_ * 8 : s_ * 8 + 8] = stats[i * 8 : i * 8 + 8]
+                psnd[4 * g + i, 0, s_ * 8 : s_ * 8 + 8] = mixed[i * 8 : i * 8 + 8].astype(bf16)
+                psnd[4 * g + i, 1, s_ * 8 : s_ * 8 + 8] = stats[at + i * 8 : at + i * 8 + 8].astype(bf16)
 
     local_copy(psnd.at[p], prcv.at[p], pr).start()
 
@@ -234,22 +244,31 @@
         hidden = hidden + orcv[k - 1].astype(f32)
     hid[...] = hidden
 
-    leaving = lax.dot_general(
-        selw[0].astype(bf16), hidden.astype(bf16), (((0,), (0,)), ((), ())), preferred_element_type=f32
-    ).astype(bf16)
-    for b in range(4):
-        dsnd[b] = leaving[:, b * 128 : (b + 1) * 128]
-
     def rows_of(o):
         return pl.ds(pl.multiple_of(o * PAIR, 2), PAIR)
 
     def chunk_rows(ch):
         return pl.ds(ch * CR, CR)
 
-    local_copy(dsnd.at[:, pl.ds(0, PAIR), :], xg.at[p, :, pl.ds(0, PAIR), :], dr.at[0]).start()
+    def each_offset(ch, body):
+        first, last = ch * CO, (ch + 1) * CO
+        if first <= SELF < last:
+            lax.fori_loop(first, SELF, body, 0)
+            lax.fori_loop(SELF + 1, last, body, 0)
+        else:
+            lax.fori_loop(first, last, body, 0)
+
+    def stays(src, dst, sems):
+        rows = pl.ds(SELF * PAIR, PAIR)
+        local_copy(src.at[:, rows, :], dst.at[:, rows, :], sems.at[SELF // CO]).start()
+
+    low_hidden = hidden.astype(bf16)
     for ch in range(NCH):
-
-        def send_rows(o, carry):
+        leaving = dot(picks[chunk_rows(ch), :], low_hidden).astype(bf16)
+        for b in range(4):
+            dsnd[b, chunk_rows(ch), :] = leaving[:, b * 128 : (b + 1) * 128]
+
+        def send_rows(o, carry, ch=ch):
             dx_, dz_ = offset_of(o)
             to = ((ex - dx_ + 4) % 4) * 8 + (ez - dz_ + 8) % 8
             remote(
@@ -257,7 +276,9 @@
             ).start()
             return carry
 
-        lax.fori_loop(max(1, ch * CO), (ch + 1) * CO, send_rows, 0)
+        each_offset(ch, send_rows)
+        if ch == SELF // CO:
+            stays(dsnd, xg.at[p], dr)
 
     def share(dy, core):
         return ((y + dy) % 4) * 2 + core
@@ -296,13 +317,21 @@
 
     local_copy(dw, dwb, lsem.at[6]).wait()
 
+    def relay(ch, then=None):
+        for dy in (1, 3, 2):
+            give(ch, (4 - dy) % 4).wait_recv()
+            pass_on(ch, dy).start()
+            if then is not None:
+                then(dy)
+
     def experts(ch):
         pass_on(ch, 0).wait_recv()
         upward(ch, partner)
-        for dy in (1, 3, 2):
-            give(ch, (4 - dy) % 4).wait_recv()
-            pass_on(ch, dy).start()
-            upward(ch, share(dy, c))
+        if ch == 0:
+            relay(ch, lambda dy: upward(ch, share(dy, c)))
+        else:
+            for dy in (1, 3, 2):
+                upward(ch, share(dy, c))
         for dy in (1, 3, 2):
             pass_on(ch, dy).wait_recv()
             upward(ch, share(dy, 1 - c))
@@ -326,14 +355,18 @@
     def home(ch, dy):
         return remote(ssnd.at[ch, dy - 1], rrcv.at[ch, dy - 1], rs.at[ch, dy - 1], rr.at[ch, dy - 1], pool=share(dy, c))
 
-    def outward(ch):
+    def lend(ch):
         for dy in (2, 1, 3, 0):
             value = down(share(dy, 1 - c)).astype(bf16)
             for b in range(4):
                 xsnd[ch, dy, b] = value[:, b * 128 : (b + 1) * 128]
             across(ch, dy).start()
+
+    def keep():
         for dy in (2, 1, 3, 0):
             part[dy] = down(share(dy, c))
+
+    def join(ch):
         for dy in (2, 1, 3, 0):
             across(ch, dy).wait_recv()
             for b in range(4):
@@ -353,8 +386,6 @@
             for dy in (1, 2, 3):
                 value = value + rrcv[ch, dy - 1, b].astype(f32)
             rsnd[b, chunk_rows(ch), :] = value.astype(bf16)
-        if ch == 0:
-            local_copy(rsnd.at[:, pl.ds(0, PAIR), :], ret.at[:, pl.ds(0, PAIR), :], tr.at[0]).start()
 
         def send_rows(o, carry):
             dx_, dz_ = offset_of(o)
@@ -362,20 +393,28 @@
             remote(rsnd.at[:, rows_of(o), :], ret.at[:, rows_of(o), :], ts.at[ch], tr.at[ch], expert=to).start()
             return carry
 
-        lax.fori_loop(max(1, ch * CO), (ch + 1) * CO, send_rows, 0)
-
-    experts(0)
-    outward(0)
-    for ch in range(1, NCH):
+        each_offset(ch, send_rows)
+        if ch == SELF // CO:
+            stays(rsnd, ret, tr)
+
+    for ch in range(NCH):
         experts(ch)
-        outward(ch)
-        back(ch - 1)
-    back(NCH - 1)
+        lend(ch)
+        if ch + 1 < NCH:
+            relay(ch + 1)
+        if ch:
+            join(ch - 1)
+        keep()
+        if ch >= 3:
+            back(ch - 3)
+    join(NCH - 1)
+    for ch in range(max(0, NCH - 3), NCH):
+        back(ch)
 
     for ch in range(NCH):
         wait_bytes(ret.at[:, chunk_rows(ch), :], tr.at[ch])
-    high = selw[1].astype(bf16)
-    low = (selw[1] - high.astype(f32)).astype(bf16)
+    high = selw[...].astype(bf16)
+    low = (selw[...] - high.astype(f32)).astype(bf16)
     returned = jnp.concatenate([ret[b] for b in range(4)], axis=1)
     summed = dot(jnp.concatenate([high, low], axis=0), returned)
     fsnd[...] = (hid[...] + (summed[0:16] + summed[16:32])).astype(bf16)
@@ -388,7 +427,7 @@
     lax.fori_loop(1, POOL, send_result, 0)
     wait_bytes(fall, er)
     for s in range(POOL):
-        out[:, :, s * 512 : (s + 1) * 512] = fall[s].reshape(8, 2, 512)
+        out[:, s * 512 : (s + 1) * 512] = fall[s]
 
     wait_bytes(qall.at[pl.ds(0, POOL - 1)], qs)
     wait_bytes(psnd.at[pl.ds(0, POOL - 1)], ps)
@@ -396,7 +435,7 @@
     for k in range(1, 8):
         remote(osnd.at[k - 1], orcv.at[k - 1], os_.at[k - 1], or_.at[k - 1], pool=p).wait_send()
     for ch in range(NCH):
-        sent = pl.ds(0, CR - PAIR if ch == 0 else CR)
+        sent = pl.ds(0, CR - PAIR if ch == SELF // CO else CR)
         wait_bytes(dsnd.at[:, sent, :], ds_.at[ch])
         wait_bytes(rsnd.at[:, sent, :], ts.at[ch])
         for dy in range(4):
@@ -416,10 +455,10 @@
     anywhere = pl.BlockSpec(memory_space=pl.ANY)
     dma = pltpu.SemaphoreType.DMA
     V = pltpu.VMEM
-    return pl.pallas_call(
+    gathered = pl.pallas_call(
         layer_kernel,
         name="layer",
-        out_shape=jax.ShapeDtypeStruct(residual.shape, bf16),
+        out_shape=jax.ShapeDtypeStruct((16, 4096), bf16),
         in_specs=[smem] * 3 + [anywhere] + [vmem] * 3 + [anywhere] * 6,
         out_specs=vmem,
         scratch_shapes=[
@@ -430,7 +469,7 @@
             V((2, 4096, 128), bf16),
             V((2, 128, 4096), bf16),
             V((8, 2, 512), bf16),
-            V((8, 8, 2, 4, 128), bf16),
+            V((8, 8, 8, 128), bf16),
             V((8, 2, 32, 128), bf16),
             V((8, 2, 32, 128), bf16),
             V((8, 8, 128), f32),
@@ -441,7 +480,9 @@
             V((7, 16, 512), bf16),
             V((7, 16, 512), bf16),
             V((16, 512), f32),
-            V((2, 16, ROWS), f32),
+            V((16, ROWS), f32),
+            V((ROWS, 16), bf16),
+            V((8, 8, 128), bf16),
             V((4, ROWS, 128), bf16),
             V((8, 4, ROWS, 128), bf16),
             V((NCH, 2, CR, 256), f32),
@@ -468,6 +509,7 @@
         cache_len, page_row.reshape(32), page_len.reshape(32), residual, queries, routes, route_weight,
         kv_cache, kv_pages, out_weight, gate_weight, up_weight, down_weight,
     )
+    return gathered.reshape(residual.shape)
 
 
 def solution(mesh):

time: 68.5 us -> 65.5 us (0.956)
  Pallas kernels: 66.7 us -> 63.5 us
    pallas_call x1, Pallas kernels: 66.7 us -> 63.5 us  [per_device(): pl.pallas_call(layer_kernel, name='layer', out_shape=jax.ShapeDtypeStruct...]
    reshape x0 -> x1, local copies, waits for them, and re-layouts: none -> 1.67 us  [per_device(): return gathered.reshape(residual.shape)]
    unnamed x1 -> x0, local copies, waits for them, and re-layouts: 1.65 us -> none
where the time goes in v2:
time: 65.5 us; the launch traced here: 65.2 us
  Pallas kernels  63.5 us (97%)
  local copies, waits for them, and re-layouts  1.67 us (3%)
    pallas_call x1, Pallas kernels, per_device(): pl.pallas_call(layer_kernel, name='layer', out_shape=jax.ShapeDtypeStruct...  63.5 us
    reshape x1, local copies, waits for them, and re-layouts, per_device(): return gathered.reshape(residual.shape)  1.67 us

profile of v2, /device:TPU:1, one launch (start us, length us, event | category | flops | bytes accessed | tf_op | source)
XLA Modules:
  0.0 65.2 jit_solution(12180506370168597193)
XLA Ops:
  0.0 63.5 %layer.1 = bf16[16,4096]{1,0:T(8,128)(2,1)} custom-call(s32[8]{0:T(128)} %clen.1, s32[32]{0:T(128)} %bitcast.2, s32[32]{0:T(128)} %bitcast.3, bf16[8,2,4096]{2,1,0:T(2,128)(2,1)} %res.1, bf16[8,2,4,128]{3,2,1,0:T(4,128)(2,1)} %q.1, s32[8,2,8]{2,1,0:T(2,128)} %routes.1, f32[8,2,8]{2,1,0:T(2,128)} %rw.1, bf16[8,512,2,2,128]{4,3,2,1,0:T(2,128)(2,1)} %kv.1, ...), custom_call_target="tpu_custom_call" | custom-call | tf_op jit(solution)/shard_map/layer/pallas_call | solution.py:458
  63.6 1.7 %reshape.11 = bf16[8,2,4096]{2,1,0:T(2,128)(2,1)} reshape(bf16[16,4096]{1,0:T(8,128)(2,1)} %layer.1) | data formatting | bytes 262144 | tf_op jit(solution)/shard_map/reshape | solution.py:512

commit v3 on v2

--- a/solution.py
+++ b/solution.py
@@ -15,6 +15,8 @@
 CAP = 3
 NCH = 4
 ROT = 2
+FAR_IN = (1, 2, 3)
+FAR_OUT = (0, 1, 2)
 ROWS = EXPERT * 2 * CAP
 CR = ROWS // NCH
 CO = EXPERT // NCH
@@ -56,8 +58,9 @@
     qall, psnd, prcv, own_m, own_top, own_tot, row_top, att,
     osnd, orcv, hid, selw, picks, q8, dsnd, xg, acc, act,
     xsnd, xrcv, part, ssnd, rrcv, fin, rsnd, ret, fsnd, fall,
+    hsnd, hfar, dsnd2, rsnd2, ret2, wsnd, wrcv,
     lsem, kvsem, qs, qr, ps, pr, os_, or_, ds_, dr, as_, ar, fs, fr,
-    xs, xr, rs, rr, ts, tr, es, er,
+    xs, xr, rs, rr, ts, tr, es, er, gs, gr, d2s, d2r, t2s, t2r, ws, wr,
 ):
     p = lax.axis_index("pool")
     e = lax.axis_index("expert")
@@ -263,22 +266,32 @@
         local_copy(src.at[:, rows, :], dst.at[:, rows, :], sems.at[SELF // CO]).start()
 
     low_hidden = hidden.astype(bf16)
-    for ch in range(NCH):
-        leaving = dot(picks[chunk_rows(ch), :], low_hidden).astype(bf16)
+    across_ring = ((y + 2) % 4) * 2 + c
+    hsnd[...] = low_hidden
+    swap = remote(hsnd, hfar, gs, gr, pool=across_ring)
+    swap.start()
+    def depart(ch, columns, held, place, ssem, rsem):
+        leaving = dot(picks[chunk_rows(ch), :], columns).astype(bf16)
         for b in range(4):
-            dsnd[b, chunk_rows(ch), :] = leaving[:, b * 128 : (b + 1) * 128]
-
-        def send_rows(o, carry, ch=ch):
+            held[b, chunk_rows(ch), :] = leaving[:, b * 128 : (b + 1) * 128]
+
+        def send_rows(o, carry):
             dx_, dz_ = offset_of(o)
             to = ((ex - dx_ + 4) % 4) * 8 + (ez - dz_ + 8) % 8
             remote(
-                dsnd.at[:, rows_of(o), :], xg.at[p, :, rows_of(o), :], ds_.at[ch], dr.at[ch], expert=to
+                held.at[:, rows_of(o), :], xg.at[place, :, rows_of(o), :], ssem.at[ch], rsem.at[ch], expert=to
             ).start()
             return carry
 
         each_offset(ch, send_rows)
         if ch == SELF // CO:
-            stays(dsnd, xg.at[p], dr)
+            stays(held, xg.at[place], rsem)
+
+    for ch in range(NCH):
+        depart(ch, low_hidden, dsnd, p, ds_, dr)
+    swap.wait_recv()
+    for ch in FAR_IN:
+        depart(ch, hfar[...], dsnd2, across_ring, d2s, d2r)
 
     def share(dy, core):
         return ((y + dy) % 4) * 2 + core
@@ -307,7 +320,7 @@
 
     for ch in range(NCH):
         wait_bytes(block_of(p, ch), dr.at[ch])
-        for dy in (1, 3, 2):
+        for dy in (1, 3) if ch in FAR_IN else (1, 3, 2):
             give(ch, dy).start()
         pass_on(ch, 0).start()
         if ch == 0:
@@ -319,7 +332,10 @@
 
     def relay(ch, then=None):
         for dy in (1, 3, 2):
-            give(ch, (4 - dy) % 4).wait_recv()
+            if dy == 2 and ch in FAR_IN:
+                wait_bytes(block_of(across_ring, ch), d2r.at[ch])
+            else:
+                give(ch, (4 - dy) % 4).wait_recv()
             pass_on(ch, dy).start()
             if then is not None:
                 then(dy)
@@ -356,46 +372,57 @@
         return remote(ssnd.at[ch, dy - 1], rrcv.at[ch, dy - 1], rs.at[ch, dy - 1], rr.at[ch, dy - 1], pool=share(dy, c))
 
     def lend(ch):
-        for dy in (2, 1, 3, 0):
-            value = down(share(dy, 1 - c)).astype(bf16)
+        order = (2, 1, 3, 0)
+        values = [down(share(dy, 1 - c)).astype(bf16) for dy in order]
+        for dy, value in zip(order, values):
             for b in range(4):
                 xsnd[ch, dy, b] = value[:, b * 128 : (b + 1) * 128]
+        for dy in order:
             across(ch, dy).start()
 
     def keep():
         for dy in (2, 1, 3, 0):
             part[dy] = down(share(dy, c))
 
+    def go_home(ch, held, place, ssem, rsem):
+        def send_rows(o, carry):
+            dx_, dz_ = offset_of(o)
+            to = ((ex + dx_) % 4) * 8 + (ez + dz_ + 8) % 8
+            remote(
+                held.at[:, rows_of(o), :], place.at[:, rows_of(o), :], ssem.at[ch], rsem.at[ch], expert=to
+            ).start()
+            return carry
+
+        each_offset(ch, send_rows)
+        if ch == SELF // CO:
+            stays(held, place, rsem)
+
     def join(ch):
-        for dy in (2, 1, 3, 0):
+        far = ch in FAR_OUT
+        for dy in (1, 3, 2, 0) if far else (2, 1, 3, 0):
             across(ch, dy).wait_recv()
             for b in range(4):
                 value = part[dy, :, b * 128 : (b + 1) * 128] + xrcv[ch, dy, b].astype(f32)
-                if dy:
+                if dy == 2 and far:
+                    rsnd2[b, chunk_rows(ch), :] = value.astype(bf16)
+                elif dy:
                     ssnd[ch, dy - 1, b] = value.astype(bf16)
                 else:
                     fin[b, chunk_rows(ch), :] = value
-            if dy:
+            if dy == 2 and far:
+                go_home(ch, rsnd2, ret2, t2s, t2r)
+            elif dy:
                 home(ch, dy).start()
 
     def back(ch):
-        for dy in (1, 3, 2):
+        for dy in (1, 3) if ch in FAR_OUT else (1, 3, 2):
             home(ch, dy).wait_recv()
         for b in range(4):
             value = fin[b, chunk_rows(ch), :]
-            for dy in (1, 2, 3):
+            for dy in (1, 3) if ch in FAR_OUT else (1, 2, 3):
                 value = value + rrcv[ch, dy - 1, b].astype(f32)
             rsnd[b, chunk_rows(ch), :] = value.astype(bf16)
-
-        def send_rows(o, carry):
-            dx_, dz_ = offset_of(o)
-            to = ((ex + dx_) % 4) * 8 + (ez + dz_ + 8) % 8
-            remote(rsnd.at[:, rows_of(o), :], ret.at[:, rows_of(o), :], ts.at[ch], tr.at[ch], expert=to).start()
-            return carry
-
-        each_offset(ch, send_rows)
-        if ch == SELF // CO:
-            stays(rsnd, ret, tr)
+        go_home(ch, rsnd, ret, ts, tr)
 
     for ch in range(NCH):
         experts(ch)
@@ -411,13 +438,25 @@
     for ch in range(max(0, NCH - 3), NCH):
         back(ch)
 
+    high = selw[...].astype(bf16)
+    low = (selw[...] - high.astype(f32)).astype(bf16)
+    both = jnp.concatenate([high, low], axis=0)
+
+    def weigh(place, rows):
+        returned = jnp.concatenate([place[b, 0:rows, :] for b in range(4)], axis=1)
+        summed = dot(both[:, 0:rows], returned)
+        return summed[0:16] + summed[16:32]
+
+    for ch in FAR_OUT:
+        wait_bytes(ret2.at[:, chunk_rows(ch), :], t2r.at[ch])
+    wsnd[...] = weigh(ret2, len(FAR_OUT) * CR).astype(bf16)
+    settle = remote(wsnd, wrcv, ws, wr, pool=across_ring)
+    settle.start()
     for ch in range(NCH):
         wait_bytes(ret.at[:, chunk_rows(ch), :], tr.at[ch])
-    high = selw[...].astype(bf16)
-    low = (selw[...] - high.astype(f32)).astype(bf16)
-    returned = jnp.concatenate([ret[b] for b in range(4)], axis=1)
-    summed = dot(jnp.concatenate([high, low], axis=0), returned)
-    fsnd[...] = (hid[...] + (summed[0:16] + summed[16:32])).astype(bf16)
+    summed = weigh(ret, ROWS)
+    settle.wait_recv()
+    fsnd[...] = (hid[...] + (summed + wrcv[...].astype(f32))).astype(bf16)
     local_copy(fsnd, fall.at[p], er).start()
 
     def send_result(k, carry):
@@ -429,6 +468,8 @@
     for s in range(POOL):
         out[:, s * 512 : (s + 1) * 512] = fall[s]
 
+    swap.wait_send()
+    settle.wait_send()
     wait_bytes(qall.at[pl.ds(0, POOL - 1)], qs)
     wait_bytes(psnd.at[pl.ds(0, POOL - 1)], ps)
     wait_bytes(fall.at[pl.ds(0, POOL - 1)], es)
@@ -438,9 +479,14 @@
         sent = pl.ds(0, CR - PAIR if ch == SELF // CO else CR)
         wait_bytes(dsnd.at[:, sent, :], ds_.at[ch])
         wait_bytes(rsnd.at[:, sent, :], ts.at[ch])
+        if ch in FAR_IN:
+            wait_bytes(dsnd2.at[:, sent, :], d2s.at[ch])
+        if ch in FAR_OUT:
+            wait_bytes(rsnd2.at[:, sent, :], t2s.at[ch])
         for dy in range(4):
-            if dy:
+            if dy and not (dy == 2 and ch in FAR_IN):
                 give(ch, dy).wait_send()
+            if dy and not (dy == 2 and ch in FAR_OUT):
                 home(ch, dy).wait_send()
             pass_on(ch, dy).wait_send()
             across(ch, dy).wait_send()
@@ -458,7 +504,7 @@
     gathered = pl.pallas_call(
         layer_kernel,
         name="layer",
-        out_shape=jax.ShapeDtypeStruct((16, 4096), bf16),
+        out_shape=pltpu.VMEM((16, 4096), bf16),
         in_specs=[smem] * 3 + [anywhere] + [vmem] * 3 + [anywhere] * 6,
         out_specs=vmem,
         scratch_shapes=[
@@ -497,10 +543,17 @@
             V((4, ROWS, 128), bf16),
             V((16, 512), bf16),
             V((8, 16, 512), bf16),
+            V((16, 512), bf16),
+            V((16, 512), bf16),
+            V((4, ROWS, 128), bf16),
+            V((4, ROWS, 128), bf16),
+            V((4, ROWS, 128), bf16),
+            V((16, 512), bf16),
+            V((16, 512), bf16),
             dma((7,)), dma((8,)), dma(()), dma(()), dma(()), dma(()), dma((7,)), dma((7,)),
             dma((NCH,)), dma((NCH,)), dma((NCH, 4)), dma((NCH, 4)), dma((NCH, 4)), dma((NCH, 4)),
             dma((NCH, 4)), dma((NCH, 4)), dma((NCH, 3)), dma((NCH, 3)), dma((NCH,)), dma((NCH,)),
-            dma(()), dma(()),
+            dma(()), dma(()), dma(()), dma(()), dma((NCH,)), dma((NCH,)), dma((NCH,)), dma((NCH,)), dma(()), dma(()),
         ],
         compiler_params=pltpu.CompilerParams(
             collective_id=0, has_side_effects=True, vmem_limit_bytes=60 * 1024 * 1024

time: 65.5 us -> 61.6 us (0.940)
  Pallas kernels: 63.5 us -> 60.7 us
  local copies, waits for them, and re-layouts: 1.67 us -> 0.76 us
    pallas_call x1, Pallas kernels: 63.5 us -> 60.7 us  [per_device(): pl.pallas_call(layer_kernel, name='layer', out_shape=pltpu.VMEM((16, 4096...]
    reshape x1, local copies, waits for them, and re-layouts: 1.67 us -> 0.76 us  [per_device(): return gathered.reshape(residual.shape)]
where the time goes in v3:
time: 61.6 us; the launch traced here: 61.5 us
  Pallas kernels  60.7 us (99%)
  local copies, waits for them, and re-layouts  0.76 us (1%)
    pallas_call x1, Pallas kernels, per_device(): pl.pallas_call(layer_kernel, name='layer', out_shape=pltpu.VMEM((16, 4096...  60.7 us

profile of v3, /device:TPU:1, one launch (start us, length us, event | category | flops | bytes accessed | tf_op | source)
XLA Modules:
  0.0 61.5 jit_solution(10042216944023396174)
XLA Ops:
  0.0 60.7 %layer.1 = bf16[16,4096]{1,0:T(8,128)(2,1)S(1)} custom-call(s32[8]{0:T(128)} %clen.1, s32[32]{0:T(128)} %bitcast.2, s32[32]{0:T(128)} %bitcast.3, bf16[8,2,4096]{2,1,0:T(2,128)(2,1)} %res.1, bf16[8,2,4,128]{3,2,1,0:T(4,128)(2,1)} %q.1, s32[8,2,8]{2,1,0:T(2,128)} %routes.1, f32[8,2,8]{2,1,0:T(2,128)} %rw.1, bf16[8,512,2,2,128]{4,3,2,1,0:T(2,128)(2,1)} %kv.1, ...), custom_call_target="tpu_custom_call" | custom-call | tf_op jit(solution)/shard_map/layer/pallas_call | solution.py:504
  60.7 0.8 %reshape.11 = bf16[8,2,4096]{2,1,0:T(2,128)(2,1)} reshape(bf16[16,4096]{1,0:T(8,128)(2,1)S(1)} %layer.1) | data formatting | bytes 262144 | tf_op jit(solution)/shard_map/reshape | solution.py:565

commit v4 on v3

--- a/solution.py
+++ b/solution.py
@@ -147,11 +147,12 @@
 
     pl.semaphore_wait(barrier, EXPERT - 1 + POOL - 1)
 
-    def send_query(k, carry):
-        remote(q8, qall.at[p], qs, qr, pool=(p + k) % POOL).start()
-        return carry
-
-    lax.fori_loop(1, POOL, send_query, 0)
+    peers = [
+        ((y + dy) % 4) * 2 + core
+        for dy, core in ((2, 1 - c), (2, c), (1, 1 - c), (3, 1 - c), (1, c), (3, c), (0, 1 - c))
+    ]
+    for to in peers:
+        remote(q8, qall.at[p], qs, qr, pool=to).start()
     local_copy(q8, qall.at[p], qr).start()
 
     for r in range(4, 8):
@@ -189,12 +190,8 @@
 
     local_copy(psnd.at[p], prcv.at[p], pr).start()
 
-    def send_parts(k, carry):
-        to = (p + k) % POOL
+    for to in peers:
         remote(psnd.at[to], prcv.at[p], ps, pr, pool=to).start()
-        return carry
-
-    lax.fori_loop(1, POOL, send_parts, 0)
     local_copy(ow, owb, lsem.at[3]).wait()
     local_copy(res.at[:, :, own_cols], resb, lsem.at[2]).wait()
     wait_bytes(prcv, pr)
@@ -232,34 +229,29 @@
         [att[pl.ds(h, 16, stride=4), :].astype(bf16) for h in range(4)], axis=1
     )
 
-    def project(k):
-        to = (p + k) % POOL
-        return to, dot(attended, owb[:, pl.ds(pl.multiple_of(to * 512, 512), 512)])
-
-    for k in (4, 3, 5, 2, 6, 1, 7):
-        to, value = project(k)
-        osnd[k - 1] = value.astype(bf16)
-        remote(osnd.at[k - 1], orcv.at[k - 1], os_.at[k - 1], or_.at[k - 1], pool=to).start()
-    _, hidden = project(0)
+    def project(to):
+        return dot(attended, owb[:, pl.ds(pl.multiple_of(to * 512, 512), 512)])
+
+    for k, to in enumerate(peers):
+        osnd[k] = project(to).astype(bf16)
+        remote(osnd.at[k], orcv.at[k], os_.at[k], or_.at[k], pool=to).start()
+    hidden = project(p)
     hidden = hidden + resb[...].reshape(16, 512).astype(f32)
-    for k in range(1, 8):
-        remote(osnd.at[k - 1], orcv.at[k - 1], os_.at[k - 1], or_.at[k - 1], pool=p).wait_recv()
-        hidden = hidden + orcv[k - 1].astype(f32)
+    for k in range(7):
+        remote(osnd.at[k], orcv.at[k], os_.at[k], or_.at[k], pool=peers[k]).wait_recv()
+        hidden = hidden + orcv[k].astype(f32)
     hid[...] = hidden
 
     def rows_of(o):
-        return pl.ds(pl.multiple_of(o * PAIR, 2), PAIR)
+        return pl.ds(o * PAIR, PAIR)
 
     def chunk_rows(ch):
         return pl.ds(ch * CR, CR)
 
     def each_offset(ch, body):
-        first, last = ch * CO, (ch + 1) * CO
-        if first <= SELF < last:
-            lax.fori_loop(first, SELF, body, 0)
-            lax.fori_loop(SELF + 1, last, body, 0)
-        else:
-            lax.fori_loop(first, last, body, 0)
+        for o in range(ch * CO, (ch + 1) * CO):
+            if o != SELF:
+                body(o, 0)
 
     def stays(src, dst, sems):
         rows = pl.ds(SELF * PAIR, PAIR)
@@ -318,15 +310,17 @@
             else:
                 acc[ch, j] += value
 
-    for ch in range(NCH):
+    def offer(ch):
         wait_bytes(block_of(p, ch), dr.at[ch])
         for dy in (1, 3) if ch in FAR_IN else (1, 3, 2):
             give(ch, dy).start()
         pass_on(ch, 0).start()
-        if ch == 0:
-            local_copy(gw, gwb, lsem.at[4]).wait()
-            local_copy(uw, uwb, lsem.at[5]).wait()
         upward(ch, p, True)
+
+    local_copy(gw, gwb, lsem.at[4]).wait()
+    local_copy(uw, uwb, lsem.at[5]).wait()
+    offer(0)
+    offer(1)
 
     local_copy(dw, dwb, lsem.at[6]).wait()
 
@@ -345,6 +339,7 @@
         upward(ch, partner)
         if ch == 0:
             relay(ch, lambda dy: upward(ch, share(dy, c)))
+            offer(2)
         else:
             for dy in (1, 3, 2):
                 upward(ch, share(dy, c))
@@ -427,6 +422,8 @@
     for ch in range(NCH):
         experts(ch)
         lend(ch)
+        if ch == 0:
+            offer(3)
         if ch + 1 < NCH:
             relay(ch + 1)
         if ch:
@@ -459,11 +456,8 @@
     fsnd[...] = (hid[...] + (summed + wrcv[...].astype(f32))).astype(bf16)
     local_copy(fsnd, fall.at[p], er).start()
 
-    def send_result(k, carry):
-        remote(fsnd, fall.at[p], es, er, pool=(p + k) % POOL).start()
-        return carry
-
-    lax.fori_loop(1, POOL, send_result, 0)
+    for to in peers:
+        remote(fsnd, fall.at[p], es, er, pool=to).start()
     wait_bytes(fall, er)
     for s in range(POOL):
         out[:, s * 512 : (s + 1) * 512] = fall[s]
@@ -473,8 +467,8 @@
     wait_bytes(qall.at[pl.ds(0, POOL - 1)], qs)
     wait_bytes(psnd.at[pl.ds(0, POOL - 1)], ps)
     wait_bytes(fall.at[pl.ds(0, POOL - 1)], es)
-    for k in range(1, 8):
-        remote(osnd.at[k - 1], orcv.at[k - 1], os_.at[k - 1], or_.at[k - 1], pool=p).wait_send()
+    for k in range(7):
+        remote(osnd.at[k], orcv.at[k], os_.at[k], or_.at[k], pool=peers[k]).wait_send()
     for ch in range(NCH):
         sent = pl.ds(0, CR - PAIR if ch == SELF // CO else CR)
         wait_bytes(dsnd.at[:, sent, :], ds_.at[ch])

time: 61.6 us -> 60.1 us (0.976)
  Pallas kernels: 60.7 us -> 59.2 us
    pallas_call x1, Pallas kernels: 60.7 us -> 59.2 us  [per_device(): pl.pallas_call(layer_kernel, name='layer', out_shape=pltpu.VMEM((16, 4096...]
where the time goes in v4:
time: 60.1 us; the launch traced here: 60 us
  Pallas kernels  59.2 us (99%)
  local copies, waits for them, and re-layouts  0.76 us (1%)
    pallas_call x1, Pallas kernels, per_device(): pl.pallas_call(layer_kernel, name='layer', out_shape=pltpu.VMEM((16, 4096...  59.2 us

profile of v4, /device:TPU:1, one launch (start us, length us, event | category | flops | bytes accessed | tf_op | source)
XLA Modules:
  0.0 60.0 jit_solution(15616199779856292598)
XLA Ops:
  0.0 59.2 %layer.1 = bf16[16,4096]{1,0:T(8,128)(2,1)S(1)} custom-call(s32[8]{0:T(128)} %clen.1, s32[32]{0:T(128)} %bitcast.2, s32[32]{0:T(128)} %bitcast.3, bf16[8,2,4096]{2,1,0:T(2,128)(2,1)} %res.1, bf16[8,2,4,128]{3,2,1,0:T(4,128)(2,1)} %q.1, s32[8,2,8]{2,1,0:T(2,128)} %routes.1, f32[8,2,8]{2,1,0:T(2,128)} %rw.1, bf16[8,512,2,2,128]{4,3,2,1,0:T(2,128)(2,1)} %kv.1, ...), custom_call_target="tpu_custom_call" | custom-call | tf_op jit(solution)/shard_map/layer/pallas_call | solution.py:498
  59.2 0.8 %reshape.11 = bf16[8,2,4096]{2,1,0:T(2,128)(2,1)} reshape(bf16[16,4096]{1,0:T(8,128)(2,1)S(1)} %layer.1) | data formatting | bytes 262144 | tf_op jit(solution)/shard_map/reshape | solution.py:559

commit v5 on v4

--- a/solution.py
+++ b/solution.py
@@ -15,7 +15,7 @@
 CAP = 3
 NCH = 4
 ROT = 2
-FAR_IN = (1, 2, 3)
+FAR_IN = (0, 1, 2, 3)
 FAR_OUT = (0, 1, 2)
 ROWS = EXPERT * 2 * CAP
 CR = ROWS // NCH

time: 60.1 us -> 60.4 us (level)
  no operation moved by 1% of the time
where the time goes in v5:
time: 60.4 us; the launch traced here: 60.2 us
  Pallas kernels  59.5 us (99%)
  local copies, waits for them, and re-layouts  0.76 us (1%)
    pallas_call x1, Pallas kernels, per_device(): pl.pallas_call(layer_kernel, name='layer', out_shape=pltpu.VMEM((16, 4096...  59.5 us

profile of v5, /device:TPU:1, one launch (start us, length us, event | category | flops | bytes accessed | tf_op | source)
XLA Modules:
  0.0 60.2 jit_solution(3493561751040423508)
XLA Ops:
  0.0 59.5 %layer.1 = bf16[16,4096]{1,0:T(8,128)(2,1)S(1)} custom-call(s32[8]{0:T(128)} %clen.1, s32[32]{0:T(128)} %bitcast.2, s32[32]{0:T(128)} %bitcast.3, bf16[8,2,4096]{2,1,0:T(2,128)(2,1)} %res.1, bf16[8,2,4,128]{3,2,1,0:T(4,128)(2,1)} %q.1, s32[8,2,8]{2,1,0:T(2,128)} %routes.1, f32[8,2,8]{2,1,0:T(2,128)} %rw.1, bf16[8,512,2,2,128]{4,3,2,1,0:T(2,128)(2,1)} %kv.1, ...), custom_call_target="tpu_custom_call" | custom-call | tf_op jit(solution)/shard_map/layer/pallas_call | solution.py:498
  59.5 0.8 %reshape.11 = bf16[8,2,4096]{2,1,0:T(2,128)(2,1)} reshape(bf16[16,4096]{1,0:T(8,128)(2,1)S(1)} %layer.1) | data formatting | bytes 262144 | tf_op jit(solution)/shard_map/reshape | solution.py:559
